TPU v7x, 256 devices: a whole 4x4x8 slice. The times are simulated.
256 devices in a mesh: tm: 8 (over z_hi, x), gx: 8 (over z_lo, core), gy: 4 (over y).
Axes of the slice: x: 4, y: 4, z: 8 (z_hi: 2, z_lo: 4; z = z_hi * 4 + z_lo), core: 2. Of those that a mesh axis runs over, the one named last changes fastest.
Arguments:
- increment: float32 [8, 137, 128, 512], P('tm', None, 'gx', 'gy'), may hold values from -6 to 6
- dual_state: float32 [8, 137, 128, 512], P('tm', None, 'gx', 'gy'), may hold values from -6 to 6
- forcing: float32 [8, 137, 128, 512], P('tm', None, 'gx', 'gy'), may hold values from -6 to 6
- gradient: float32 [8, 137, 128, 512], P('tm', None, 'gx', 'gy'), may hold values from -3 to 3
- courant_x: float32 [8, 137, 128, 512], P('tm', None, 'gx', 'gy'), may hold values from 0.05 to 0.3
- courant_y: float32 [8, 137, 128, 512], P('tm', None, 'gx', 'gy'), may hold values from 0.05 to 0.3
- error_var: float32 [8, 137, 128, 512], P('tm', None, 'gx', 'gy'), may hold values from 0.2 to 2
- obs_weight: float32 [8, 137, 128, 512], P('tm', None, 'gx', 'gy'), may hold values from 0.2 to 2
- diffusion: float32 [137], replicated, may hold values from 0.02 to 0.1
- level_mix: float32 [137, 137], replicated, may hold values from -0.5 to 0.8
Outputs:
- dual_next: float32 [8, 137, 128, 512], P('tm', None, 'gx', 'gy')
- increment_next: float32 [8, 137, 128, 512], P('tm', None, 'gx', 'gy')
All inputs are finite; a program needn't handle non-finite values.
Results may differ from a plain program's by a relative error of at most 0.0001.
Values sent between devices are 32-bit elements; how exact they have to be, the bound alone decides.
A program may use at most 128 MiB of HBM per device.

v0:
```python
import functools

import jax
import jax.numpy as jnp
from jax import lax
from jax.experimental import pallas as pl
from jax.experimental.pallas import tpu as pltpu
from jax.sharding import PartitionSpec as P

STEPS = 3
F32 = jnp.float32
BF16 = jnp.bfloat16
LANES = 128
MESH = pl.DeviceIdType.MESH


class Sizes:
    def __init__(self, mesh, levels, planes):
        self.tm, self.gx, self.gy = (mesh.shape[a] for a in ("tm", "gx", "gy"))
        self.xs = self.tm // 2
        self.levels = levels
        self.planes = planes
        self.rows = -(-levels // 16) * 16
        self.depth = 3 * self.rows


def kernel(
    sz,
    inc_h, dual_h, forc_h, grad_h, cx_h, cy_h, ev_h, ob_h, diff_r, mix_r,
    out_dual, out_incr,
    inc, dual, forc, grad, cx, cy, ev, ob,
    later, earlier, end,
    ca, cb, cc, sb, state, packs, halos, xsend, bpack, bhalo, asend,
    wcat, tb, stage_a, stage_b,
    load_sem, store_sem, d_send, d_recv, e_send, e_recv, h_send, h_recv, r_send, p_send, p_recv,
):
    NP, R, L = sz.planes, sz.rows, sz.levels
    XS = sz.xs
    t, g, y = (lax.axis_index(a) for a in ("tm", "gx", "gy"))
    xc, zh = lax.rem(t, XS), lax.div(t, XS)
    core, zl = lax.rem(g, 2), lax.div(g, 2)
    last_t = sz.tm - 1
    zchips = sz.gx // 2
    half = NP // 2

    def rdma(src, dst, ssem, rsem, **where):
        return pltpu.make_async_remote_copy(
            src_ref=src, dst_ref=dst, send_sem=ssem, recv_sem=rsem, device_id=where, device_id_type=MESH
        )

    def wait(ref, sem):
        pltpu.make_async_copy(ref, ref, sem).wait()

    hbm = (inc_h, cx_h, cy_h, dual_h, forc_h, ev_h, ob_h, grad_h)
    local = (inc, cx, cy, dual, forc, ev, ob, grad)
    valid = pl.ds(0, L)

    def load(i, x):
        return pltpu.make_async_copy(hbm[i].at[0, :, x, :], local[i].at[x, valid, :], load_sem.at[i, x])

    for x in range(NP):
        for i in range(3):
            load(i, x).start()
    for i in range(3, 8):
        for x in range(NP):
            load(i, x).start()

    barrier = pltpu.get_barrier_semaphore()
    group_a = [(dx, dy, dc) for dx in range(XS) for dy in range(sz.gy) for dc in range(2)][1:]
    group_b = [(dh, dl) for dh in range(2) for dl in range(zchips)][1:]

    def peer_a(dx, dy, dc):
        return {
            "tm": zh * XS + lax.rem(xc + dx, XS),
            "gy": lax.rem(y + dy, sz.gy),
            "gx": zl * 2 + lax.rem(core + dc, 2),
        }

    def peer_b(dh, dl):
        return {"tm": lax.rem(zh + dh, 2) * XS + xc, "gx": lax.rem(zl + dl, zchips) * 2 + core}

    def greet(where):
        pl.semaphore_signal(barrier, inc=1, device_id=where, device_id_type=MESH)

    for p in group_a:
        greet(peer_a(*p))
    for p in group_b:
        greet(peer_b(*p))
    outward = jnp.where(core == 0, g - 1, g + 1)
    has_out = (outward >= 0) & (outward < sz.gx)

    @pl.when(has_out)
    def _():
        greet({"gx": outward})

    across = (t == XS - 1) | (t == XS)

    @pl.when(across)
    def _():
        greet({"tm": 2 * XS - 1 - t})

    lane = lax.broadcasted_iota(jnp.int32, (8, LANES), 1)

    def at_lane(k, n):
        return jnp.broadcast_to((lane == k % LANES)[None], (n // 8, 8, LANES)).reshape(n, LANES)

    chunks = [(r, min(48, R - r)) for r in range(0, R, 48)]

    lifted = jnp.concatenate([diff_r[...], jnp.zeros((1, 2 * LANES - L), F32)], axis=1)
    turned = jnp.broadcast_to(lifted, (LANES, 2 * LANES)).T
    sb[...] = turned[:R]

    def widen(m):
        high = m.astype(BF16).astype(F32)
        low = m - high
        tail = jnp.where(lane[:1] < R - LANES, high[:, LANES:], 0.0)
        tail_low = jnp.where(lane[:1] < R - LANES, low[:, LANES:], 0.0)
        k = R - LANES
        tails = tail + pltpu.roll(tail, k, 1) + pltpu.roll(tail_low, 2 * k, 1)
        whole = jnp.concatenate([high[:, :LANES], high[:, :LANES], low[:, :LANES], tails], axis=1)
        return whole[:, : sz.depth].astype(BF16)

    mix = jnp.concatenate([mix_r[...], jnp.zeros((L, 2 * LANES - L), F32)], axis=1)
    mix = jnp.concatenate([mix, jnp.zeros((2 * LANES - L, 2 * LANES), F32)], axis=0)
    wcat[0] = widen(mix[:R])
    wcat[1] = widen(mix.T[:R])

    row = lax.broadcasted_iota(jnp.int32, (R, LANES), 0)

    def clean(v, r, n):
        return v if r + n <= L else jnp.where(row[r : r + n] < L, v, 0.0)

    @pl.when(g == 0)
    def _():
        for k in range(2 * STEPS):
            state[k, 0] = jnp.zeros((R, LANES), F32)
        ca[0] = jnp.zeros((R, LANES), F32)

    @pl.when(g == sz.gx - 1)
    def _():
        for k in range(2 * STEPS):
            state[k, NP + 1] = jnp.zeros((R, LANES), F32)

    @pl.when(y == 0)
    def _():
        for k in range(2 * STEPS):
            halos[k, 0] = jnp.zeros((R, LANES), F32)
        bhalo[...] = jnp.zeros((R, LANES), F32)

    @pl.when(y == sz.gy - 1)
    def _():
        for k in range(2 * STEPS):
            halos[k, 1] = jnp.zeros((R, LANES), F32)

    def keep(k, x, r, n, v):
        rows = pl.ds(r, n)
        state[k, x + 1, rows, :] = v
        pltpu.store(packs.at[k, 0, rows, :], v, mask=at_lane(x - 1, n))
        pltpu.store(packs.at[k, 1, rows, :], v, mask=at_lane(x, n))
        if x == 0:
            xsend[k, 0, rows, :] = pltpu.roll(v, NP, 1)
        if x == NP - 1:
            xsend[k, 1, rows, :] = pltpu.roll(v, LANES - NP, 1)

    def halo_copies(k):
        return (
            (g > 0, rdma(xsend.at[k, 0], state.at[k, NP + 1], h_send.at[k, 0], h_recv.at[k, 0], gx=g - 1)),
            (g < sz.gx - 1, rdma(xsend.at[k, 1], state.at[k, 0], h_send.at[k, 1], h_recv.at[k, 1], gx=g + 1)),
            (y < sz.gy - 1, rdma(packs.at[k, 0], halos.at[k, 0], h_send.at[k, 2], h_recv.at[k, 2], gy=y + 1)),
            (y > 0, rdma(packs.at[k, 1], halos.at[k, 1], h_send.at[k, 3], h_recv.at[k, 3], gy=y - 1)),
        )

    def send_halos(k):
        for on, copy in halo_copies(k):
            @pl.when(on)
            def _():
                copy.start()

    def recv_halos(k):
        for on, ref, i in (
            (g < sz.gx - 1, state.at[k, NP + 1], 0),
            (g > 0, state.at[k, 0], 1),
            (y > 0, halos.at[k, 0], 2),
            (y < sz.gy - 1, halos.at[k, 1], 3),
        ):
            @pl.when(on)
            def _():
                wait(ref, h_recv.at[k, i])

    def drain_halos(k):
        for on, copy in halo_copies(k):
            @pl.when(on)
            def _():
                copy.wait_send()

    coef_copies = (
        (g < sz.gx - 1, rdma(asend, ca.at[0], r_send.at[0], r_send.at[2], gx=g + 1)),
        (y < sz.gy - 1, rdma(bpack, bhalo, r_send.at[1], r_send.at[3], gy=y + 1)),
    )
    runs = t != last_t

    @pl.when(runs)
    def _():
        for x in range(NP):
            for i in range(3):
                load(i, x).wait()
            for r, n in chunks:
                rows = pl.ds(r, n)
                s = sb[rows, :]
                a = clean(pltpu.roll(cx[x, rows, :], x, 1) + s, r, n)
                b = clean(pltpu.roll(cy[x, rows, :], x, 1) + s, r, n)
                ca[x + 1, rows, :] = a
                cb[x, rows, :] = b
                cc[x, rows, :] = 1.0 - 2.0 * s - a - b
                pltpu.store(bpack.at[rows, :], b, mask=at_lane(x - 1, n))
                if x == NP - 1:
                    asend[rows, :] = pltpu.roll(a, LANES - NP, 1)
                keep(0, x, r, n, clean(pltpu.roll(inc[x, rows, :], x, 1), r, n))

    @pl.when(t == last_t)
    def _():
        for x in range(NP):
            for i in range(3):
                load(i, x).wait()

    pl.semaphore_wait(barrier, len(group_a) + len(group_b) + has_out.astype(jnp.int32) + across.astype(jnp.int32))

    @pl.when(runs)
    def _():
        send_halos(0)
        for on, copy in coef_copies:
            @pl.when(on)
            def _():
                copy.start()

    def d_copy(x):
        to = t - 1
        if x >= half:
            to = jnp.where(t == XS, last_t, to)
        return rdma(dual.at[x, valid, :], later.at[x, valid, :], d_send.at[x], d_recv.at[x], tm=to)

    def d_pass(x):
        return rdma(later.at[x, valid, :], later.at[x, valid, :], d_send.at[NP + x], d_recv.at[x], tm=XS - 1)

    for x in range(NP):
        load(3, x).wait()

        @pl.when(t > 0)
        def _():
            d_copy(x).start()

    @pl.when(t == last_t)
    def _():
        for x in range(half, NP):
            wait(later.at[x, valid, :], d_recv.at[x])
            d_pass(x).start()

    def mixed(which, pair, emit):
        out = jnp.dot(wcat[which], tb[pair], preferred_element_type=F32)
        for j in range(2):
            for r, n in chunks:
                emit(2 * pair + j, r, n, out[r : r + n, j * LANES : (j + 1) * LANES])

    def put(pair, j, r, n, v):
        high = v.astype(BF16)
        low = (v - high.astype(F32)).astype(BF16)
        cols = pl.ds(j * LANES, LANES)
        tail = R - LANES
        main = min(n, LANES - r)
        if main > 0:
            tb[pair, pl.ds(r, main), cols] = high[:main]
            tb[pair, pl.ds(LANES + r, main), cols] = low[:main]
            tb[pair, pl.ds(2 * LANES + r, main), cols] = high[:main]
        if main < n:
            m = max(main, 0)
            o = 3 * LANES + r + m - LANES
            tb[pair, pl.ds(o, n - m), cols] = high[m:]
            tb[pair, pl.ds(o + tail, n - m), cols] = low[m:]
            tb[pair, pl.ds(o + 2 * tail, n - m), cols] = high[m:]

    def tangent(k, x, r, n):
        rows = pl.ds(r, n)
        v = state[k, x + 1, rows, :]
        edge = bhalo[rows, :] * halos[k, 0, rows, :]
        from_low = ca[x, rows, :] * state[k, x, rows, :] + jnp.where(at_lane(x - 1, n), edge, cb[x, rows, :] * v)
        from_high = state[k, x + 2, rows, :] + jnp.where(at_lane(x, n), halos[k, 1, rows, :], v)
        return cc[x, rows, :] * v + pltpu.roll(from_low, 1, 1) + sb[rows, :] * pltpu.roll(from_high, LANES - 1, 1)

    def adjoint(k, x, r, n):
        rows = pl.ds(r, n)
        w = state[k, x + 1, rows, :]
        low = state[k, x, rows, :] + jnp.where(at_lane(x - 1, n), halos[k, 0, rows, :], w)
        up_x = pltpu.roll(state[k, x + 2, rows, :], LANES - 1, 1)
        up_y = pltpu.roll(jnp.where(at_lane(x, n), halos[k, 1, rows, :], w), LANES - 1, 1)
        out = cc[x, rows, :] * w + ca[x + 1, rows, :] * up_x + cb[x, rows, :] * up_y
        return out + sb[rows, :] * pltpu.roll(low, 1, 1)

    def e_copy(x):
        to = t + 1
        if x >= half:
            to = jnp.where(t == XS - 1, 0, to)
        return rdma(end.at[x, valid, :], earlier.at[x, valid, :], e_send.at[x], e_recv.at[x], tm=to)

    def e_pass(x):
        return rdma(earlier.at[x, valid, :], earlier.at[x, valid, :], e_send.at[NP + x], e_recv.at[x], tm=XS)

    def keep_end(x, r, n, v):
        end[x, pl.ds(r, n), :] = pltpu.roll(v, (LANES - x) % LANES, 1)

    @pl.when(runs)
    def _():
        for k in range(STEPS):
            recv_halos(k)
            if k == 0:
                @pl.when(g > 0)
                def _():
                    wait(ca.at[0], r_send.at[2])

                @pl.when(y > 0)
                def _():
                    wait(bhalo, r_send.at[3])
            for pair in range(half):
                for j in range(2):
                    for r, n in chunks:
                        put(pair, j, r, n, tangent(k, 2 * pair + j, r, n))
                mixed(0, pair, functools.partial(keep, k + 1) if k < STEPS - 1 else keep_end)
                if k == STEPS - 1 and pair > 0:
                    e_copy(2 * pair - 2).start()
                    e_copy(2 * pair - 1).start()
            if k < STEPS - 1:
                send_halos(k + 1)
        e_copy(NP - 2).start()
        e_copy(NP - 1).start()

    @pl.when(t == 0)
    def _():
        for x in range(half, NP):
            wait(earlier.at[x, valid, :], e_recv.at[x])
            e_pass(x).start()

    for i in range(4, 8):
        for x in range(NP):
            load(i, x).wait()
    for x in range(NP):
        for r, n in chunks:
            rows = pl.ds(r, n)
            forc[x, rows, :] = forc[x, rows, :] - ev[x, rows, :] * dual[x, rows, :] - inc[x, rows, :]
            grad[x, rows, :] = grad[x, rows, :] - ob[x, rows, :] * inc[x, rows, :] - dual[x, rows, :]

    @pl.when(runs)
    def _():
        for k in range(STEPS, 2 * STEPS):
            for pair in range(half):
                for j in range(2):
                    x = 2 * pair + j
                    if k == STEPS:
                        wait(later.at[x, valid, :], d_recv.at[x])
                    for r, n in chunks:
                        if k == STEPS:
                            v = clean(pltpu.roll(later[x, pl.ds(r, n), :], x, 1), r, n)
                        else:
                            v = adjoint(k - 1, x, r, n)
                        put(pair, j, r, n, v)
                mixed(1, pair, functools.partial(keep, k))
            send_halos(k)
            recv_halos(k)
        for x in range(NP):
            for r, n in chunks:
                rows = pl.ds(r, n)
                back = adjoint(2 * STEPS - 1, x, r, n)
                grad[x, rows, :] = grad[x, rows, :] + pltpu.roll(back, (LANES - x) % LANES, 1)

    def squares(ref, x, total):
        for r, n in chunks:
            v = clean(ref[x, pl.ds(r, n), :], r, n)
            total = total + jnp.sum((v * v).reshape(n // 8, 8, LANES), axis=0)
        return total

    total = jnp.zeros((8, LANES), F32)
    for x in range(NP):
        total = squares(grad, x, total)

    @pl.when(t > 0)
    def _():
        for x in range(NP):
            wait(earlier.at[x, valid, :], e_recv.at[x])
            for r, n in chunks:
                rows = pl.ds(r, n)
                forc[x, rows, :] = forc[x, rows, :] + earlier[x, rows, :]

    for x in range(NP):
        total = squares(forc, x, total)

    stage_a[0] = total
    for i, p in enumerate(group_a):
        rdma(stage_a.at[0], stage_a.at[i + 1], p_send.at[0], p_recv.at[0], **peer_a(*p)).start()
    everyone = stage_a.at[pl.ds(1, len(group_a))]
    wait(everyone, p_recv.at[0])
    stage_b[0] = jnp.sum(stage_a[...], axis=0)
    for i, p in enumerate(group_b):
        rdma(stage_b.at[0], stage_b.at[i + 1], p_send.at[1], p_recv.at[1], **peer_b(*p)).start()
    everyone_b = stage_b.at[pl.ds(1, len(group_b))]
    wait(everyone_b, p_recv.at[1])
    global_sum = jnp.sum(jnp.sum(stage_b[...], axis=0), keepdims=True)
    count = 2 * L * NP * LANES * sz.tm * sz.gx * sz.gy
    root_mean = jnp.sqrt(global_sum / count + 1e-06)
    scale = jnp.minimum(1.0, 0.5 / root_mean)

    outs = []
    for x in range(NP):
        for r, n in chunks:
            rows = pl.ds(r, n)
            forc[x, rows, :] = dual[x, rows, :] + scale * forc[x, rows, :]
            grad[x, rows, :] = inc[x, rows, :] + scale * grad[x, rows, :]
        for i, (ref, out) in enumerate(((forc, out_dual), (grad, out_incr))):
            copy = pltpu.make_async_copy(ref.at[x, valid, :], out.at[0, :, x, :], store_sem.at[i, x])
            copy.start()
            outs.append(copy)

    wait(everyone, p_send.at[0])
    wait(everyone_b, p_send.at[1])

    @pl.when(runs)
    def _():
        for k in range(2 * STEPS):
            drain_halos(k)
        for on, copy in coef_copies:
            @pl.when(on)
            def _():
                copy.wait_send()
        for x in range(NP):
            e_copy(x).wait_send()

    @pl.when(t > 0)
    def _():
        for x in range(NP):
            d_copy(x).wait_send()

    @pl.when(t == last_t)
    def _():
        for x in range(half, NP):
            d_pass(x).wait_send()

    @pl.when(t == 0)
    def _():
        for x in range(half, NP):
            e_pass(x).wait_send()

    for copy in outs:
        copy.wait()


def solution(mesh):
    def local(increment, dual_state, forcing, gradient, courant_x, courant_y, error_var, obs_weight, diffusion, level_mix):
        _, levels, planes, lanes = increment.shape
        assert lanes == LANES
        sz = Sizes(mesh, levels, planes)
        R = sz.rows
        field = pltpu.VMEM((planes, R, LANES), F32)
        plane = pltpu.VMEM((R, LANES), F32)
        n = 2 * STEPS
        dma = pltpu.SemaphoreType.DMA
        any_spec = pl.BlockSpec(memory_space=pltpu.HBM)
        vmem_spec = pl.BlockSpec(memory_space=pltpu.VMEM)
        block = jax.ShapeDtypeStruct(increment.shape, F32)
        return pl.pallas_call(
            functools.partial(kernel, sz),
            name="saddle",
            out_shape=[block, block],
            in_specs=[any_spec] * 8 + [vmem_spec] * 2,
            out_specs=[any_spec] * 2,
            scratch_shapes=[field] * 11
            + [
                pltpu.VMEM((planes + 1, R, LANES), F32),
                field,
                field,
                plane,
                pltpu.VMEM((n, planes + 2, R, LANES), F32),
                pltpu.VMEM((n, 2, R, LANES), F32),
                pltpu.VMEM((n, 2, R, LANES), F32),
                pltpu.VMEM((n, 2, R, LANES), F32),
                plane,
                plane,
                plane,
                pltpu.VMEM((2, R, sz.depth), BF16),
                pltpu.VMEM((planes // 2, sz.depth, 2 * LANES), BF16),
                pltpu.VMEM((sz.xs * sz.gy * 2, 8, LANES), F32),
                pltpu.VMEM((sz.gx, 8, LANES), F32),
                dma((8, planes)),
                dma((2, planes)),
                dma((2 * planes,)),
                dma((planes,)),
                dma((2 * planes,)),
                dma((planes,)),
                dma((n, 4)),
                dma((n, 4)),
                dma((4,)),
                dma((2,)),
                dma((2,)),
            ],
            compiler_params=pltpu.CompilerParams(
                collective_id=0, has_side_effects=True, vmem_limit_bytes=60 * 1024 * 1024
            ),
        )(
            increment, dual_state, forcing, gradient, courant_x, courant_y, error_var, obs_weight,
            diffusion.reshape(1, -1), level_mix,
        )

    spec = P("tm", None, "gx", "gy")
    return jax.shard_map(
        local,
        mesh=mesh,
        in_specs=(spec,) * 8 + (P(), P()),
        out_specs=(spec, spec),
        check_vma=False,
    )
```

profile of v0, /device:TPU:1, one launch (start us, length us, event | category | flops | bytes accessed | tf_op | source)
XLA Modules:
  0.0 88.1 jit_solution(4828461196108195094)
XLA Ops:
  0.6 84.0 %saddle.1 = (f32[1,137,16,128]{3,2,1,0:T(8,128)}, f32[1,137,16,128]{3,2,1,0:T(8,128)}) custom-call(f32[1,137,16,128]{3,2,1,0:T(8,128)} %inc_h.1, f32[1,137,16,128]{3,2,1,0:T(8,128)} %dual_h.1, f32[1,137,16,128]{3,2,1,0:T(8,128)} %forc_h.1, f32[1,137,16,128]{3,2,1,0:T(8,128)} %grad_h.1, f32[1,137,16,128]{3,2,1,0:T(8,128)} %cx_h.1, f32[1,137,16,128]{3,2,1,0:T(8,128)} %cy_h.1, ...), custom_call_target="tpu_custom_call" | custom-call | tf_op jit(solution)/shard_map/saddle/pallas_call | solution.py:466
  84.7 0.0 copy-start
  84.7 2.4 %copy.14 = f32[1,137,16,128]{3,2,1,0:T(8,128)} copy(f32[1,137,16,128]{3,2,1,0:T(8,128)} %get-tuple-element.4) | data formatting | bytes 2244608
  87.1 0.0 copy-done
  87.1 1.0 %copy.15 = f32[1,137,16,128]{3,2,1,0:T(8,128)} copy(f32[1,137,16,128]{3,2,1,0:T(8,128)S(1)} %copy-done) | data formatting | bytes 2244608
Async XLA Ops:
  84.7 2.4 %copy-start = (f32[1,137,16,128]{3,2,1,0:T(8,128)S(1)}, f32[1,137,16,128]{3,2,1,0:T(8,128)}, u32[]{:S(2)}) copy-start(f32[1,137,16,128]{3,2,1,0:T(8,128)} %get-tuple-element.5) | copy-start | bytes 3366916
where the time goes:
time: 88.6 us; the launch traced here: 88.1 us
  Pallas kernels  84 us (95%)
  local copies, waits for them, and re-layouts  3.41 us (4%)
    pallas_call x1, Pallas kernels, local(): pl.pallas_call(functools.partial(kernel, sz), name='saddle', out_shape=[b...  84 us
    unnamed x4, local copies, waits for them, and re-layouts  3.41 us

commit v1 on v0

v1 whole, which is shorter than its diff:
```python
import functools

import jax
import jax.numpy as jnp
from jax import lax
from jax.experimental import pallas as pl
from jax.experimental.pallas import tpu as pltpu
from jax.sharding import PartitionSpec as P

STEPS = 3
F32 = jnp.float32
BF16 = jnp.bfloat16
LANES = 128
MESH = pl.DeviceIdType.MESH


class Sizes:
    def __init__(self, mesh, levels, planes):
        self.tm, self.gx, self.gy = (mesh.shape[a] for a in ("tm", "gx", "gy"))
        self.xs = self.tm // 2
        self.levels = levels
        self.planes = planes
        self.rows = -(-levels // 16) * 16
        self.depth = 3 * self.rows


def kernel(
    sz,
    inc_h, dual_h, forc_h, grad_h, cx_h, cy_h, ev_h, ob_h, diff_h, mix_h,
    forc, grad, dual, inc, sums,
    cx, cy, ev, ob,
    later, earlier, end, side, acc,
    ca, cb, cc, sb, state, slim_out, slim_in, edges, xsend, bslim_out, bslim_in, bhalo, asend,
    diff_r, mix_r, wcat, tb, stage_a, stage_b,
    load_sem, d_send, d_recv, s_recv, e_send, e_recv, h_send, h_recv, c_send, c_recv, p_send, p_recv,
):
    NP, R, L = sz.planes, sz.rows, sz.levels
    XS = sz.xs
    t, g, y = (lax.axis_index(a) for a in ("tm", "gx", "gy"))
    xc, zh = lax.rem(t, XS), lax.div(t, XS)
    core, zl = lax.rem(g, 2), lax.div(g, 2)
    last_t = sz.tm - 1
    zchips = sz.gx // 2
    half = NP // 2
    scope = jax.named_scope

    def rdma(src, dst, ssem, rsem, **where):
        return pltpu.make_async_remote_copy(
            src_ref=src, dst_ref=dst, send_sem=ssem, recv_sem=rsem, device_id=where, device_id_type=MESH
        )

    def wait(ref, sem):
        pltpu.make_async_copy(ref, ref, sem).wait()

    barrier = pltpu.get_barrier_semaphore()
    group_a = [(dx, dy, dc) for dx in range(XS) for dy in range(sz.gy) for dc in range(2)][1:]
    group_b = [(dh, dl) for dh in range(2) for dl in range(zchips)][1:]

    def peer_a(dx, dy, dc):
        return {
            "tm": zh * XS + lax.rem(xc + dx, XS),
            "gy": lax.rem(y + dy, sz.gy),
            "gx": zl * 2 + lax.rem(core + dc, 2),
        }

    def peer_b(dh, dl):
        return {"tm": lax.rem(zh + dh, 2) * XS + xc, "gx": lax.rem(zl + dl, zchips) * 2 + core}

    def greet(where):
        pl.semaphore_signal(barrier, inc=1, device_id=where, device_id_type=MESH)

    for p in group_b:
        greet(peer_b(*p))
    for p in group_a:
        greet(peer_a(*p))
    outward = jnp.where(core == 0, g - 1, g + 1)
    has_out = (outward >= 0) & (outward < sz.gx)

    @pl.when(has_out)
    def _():
        greet({"gx": outward})

    across = jnp.where(t == XS - 1, 2, jnp.where((t == XS) | (t == XS + 1), 1, 0))

    @pl.when(t == XS - 1)
    def _():
        greet({"tm": XS})
        greet({"tm": XS + 1})

    @pl.when((t == XS) | (t == XS + 1))
    def _():
        greet({"tm": XS - 1})

    hbm = (inc_h, cx_h, cy_h, dual_h, forc_h, ev_h, ob_h, grad_h)
    local = (inc, cx, cy, dual, forc, ev, ob, grad)
    valid = pl.ds(0, L)

    def load(i):
        for x in range(NP):
            pltpu.make_async_copy(hbm[i].at[0, :, x, :], local[i].at[x, valid, :], load_sem.at[i]).start()

    def loaded(i):
        wait(local[i].at[:, valid, :], load_sem.at[i])

    diff_copy = pltpu.make_async_copy(diff_h, diff_r, load_sem.at[8])
    mix_copy = pltpu.make_async_copy(mix_h, mix_r, load_sem.at[9])
    diff_copy.start()
    for i in range(4):
        load(i)
    mix_copy.start()

    lane = lax.broadcasted_iota(jnp.int32, (8, LANES), 1)

    def at_lane(k, n):
        return jnp.broadcast_to((lane == k % LANES)[None], (n // 8, 8, LANES)).reshape(n, LANES)

    chunks = [(r, min(48, R - r)) for r in range(0, R, 48)]

    diff_copy.wait()
    lifted = jnp.concatenate([diff_r[...], jnp.zeros((1, 2 * LANES - L), F32)], axis=1)
    turned = jnp.broadcast_to(lifted, (LANES, 2 * LANES)).T
    sb[...] = turned[:R]

    def widen(m):
        high = m.astype(BF16).astype(F32)
        low = m - high
        tail = jnp.where(lane[:1] < R - LANES, high[:, LANES:], 0.0)
        tail_low = jnp.where(lane[:1] < R - LANES, low[:, LANES:], 0.0)
        k = R - LANES
        tails = tail + pltpu.roll(tail, k, 1) + pltpu.roll(tail_low, 2 * k, 1)
        whole = jnp.concatenate([high[:, :LANES], high[:, :LANES], low[:, :LANES], tails], axis=1)
        return whole[:, : sz.depth].astype(BF16)

    row = lax.broadcasted_iota(jnp.int32, (R, LANES), 0)

    def clean(v, r, n):
        return v if r + n <= L else jnp.where(row[r : r + n] < L, v, 0.0)

    @pl.when(g == 0)
    def _():
        for k in range(2 * STEPS):
            state[k, 0] = jnp.zeros((R, LANES), F32)
        ca[0] = jnp.zeros((R, LANES), F32)

    @pl.when(g == sz.gx - 1)
    def _():
        for k in range(2 * STEPS):
            state[k, NP + 1] = jnp.zeros((R, LANES), F32)

    @pl.when(y == 0)
    def _():
        for k in range(2 * STEPS):
            slim_in[k, 0] = jnp.zeros(slim_in.shape[2:], F32)
        bslim_in[...] = jnp.zeros(bslim_in.shape, F32)

    @pl.when(y == sz.gy - 1)
    def _():
        for k in range(2 * STEPS):
            slim_in[k, 1] = jnp.zeros(slim_in.shape[2:], F32)

    share = LANES // NP

    def slim(planes, dst, sides):
        for o in range(0, R // 8, share):
            acc = {}
            for j in range(min(share, R // 8 - o)):
                rows = pl.ds(8 * (o + j), 8)
                part = {}
                for x in range(NP):
                    v = planes(x, rows)
                    for side in sides:
                        part[side] = jnp.where(lane == (x + side - 1) % LANES, v, part[side]) if x else v
                for side in sides:
                    if j:
                        turned = pltpu.roll(part[side], NP * j, 1)
                        inside = (lane >= NP * j + side - 1) & (lane < NP * (j + 1) + side - 1)
                        acc[side] = jnp.where(inside, turned, acc[side])
                    else:
                        acc[side] = part[side]
            for side in sides:
                dst(side)[pl.ds(8 * (o // share), 8), :] = acc[side]

    def unslim(src, i):
        tile = src[pl.ds(8 * (i // share), 8), :]
        j = i % share
        return pltpu.roll(tile, LANES - NP * j, 1) if j else tile

    def keep(k, x, r, n, v):
        rows = pl.ds(r, n)
        state[k, x + 1, rows, :] = v
        if x == 0:
            xsend[k, 0, rows, :] = pltpu.roll(v, NP, 1)
        if x == NP - 1:
            xsend[k, 1, rows, :] = pltpu.roll(v, LANES - NP, 1)

    def halo_copies(k):
        return (
            (g > 0, xsend.at[k, 0], state.at[k, NP + 1], h_send.at[k, 0], h_recv.at[k, 0], {"gx": g - 1}),
            (g < sz.gx - 1, xsend.at[k, 1], state.at[k, 0], h_send.at[k, 1], h_recv.at[k, 1], {"gx": g + 1}),
            (y < sz.gy - 1, slim_out.at[k, 0], slim_in.at[k, 0], h_send.at[k, 2], h_recv.at[k, 2], {"gy": y + 1}),
            (y > 0, slim_out.at[k, 1], slim_in.at[k, 1], h_send.at[k, 3], h_recv.at[k, 3], {"gy": y - 1}),
        )

    def each(copies, act):
        for on, src, dst, ssem, rsem, where in copies:
            @pl.when(on)
            def _():
                act(rdma(src, dst, ssem, rsem, **where))

    def send_x(k):
        each(halo_copies(k)[:2], lambda c: c.start())

    def send_y(k):
        slim(lambda x, rows: state[k, x + 1, rows, :], lambda side: slim_out.at[k, side], (0, 1))
        each(halo_copies(k)[2:], lambda c: c.start())

    def recv_x(k):
        for on, ref, i in ((g < sz.gx - 1, state.at[k, NP + 1], 0), (g > 0, state.at[k, 0], 1)):
            @pl.when(on)
            def _():
                wait(ref, h_recv.at[k, i])

    def recv_y(k):
        for on, ref, i in ((y > 0, slim_in.at[k, 0], 2), (y < sz.gy - 1, slim_in.at[k, 1], 3)):
            @pl.when(on)
            def _():
                wait(ref, h_recv.at[k, i])
        for i in range(R // 8):
            rows = pl.ds(8 * i, 8)
            low = unslim(slim_in.at[k, 0], i)
            edges[0, rows, :] = bhalo[rows, :] * low if k < STEPS else low
            edges[1, rows, :] = unslim(slim_in.at[k, 1], i)

    coef_copies = (
        (g < sz.gx - 1, asend, ca.at[0], c_send.at[0], c_recv.at[0], {"gx": g + 1}),
        (y < sz.gy - 1, bslim_out, bslim_in, c_send.at[1], c_recv.at[1], {"gy": y + 1}),
    )
    runs = t != last_t
    for i in range(3):
        loaded(i)

    @pl.when(runs)
    def _():
        for x in range(NP):
            for r, n in chunks:
                rows = pl.ds(r, n)
                s = sb[rows, :]
                a = clean(pltpu.roll(cx[x, rows, :], x, 1) + s, r, n)
                b = clean(pltpu.roll(cy[x, rows, :], x, 1) + s, r, n)
                ca[x + 1, rows, :] = a
                cb[x, rows, :] = b
                cc[x, rows, :] = 1.0 - 2.0 * s - a - b
                if x == NP - 1:
                    asend[rows, :] = pltpu.roll(a, LANES - NP, 1)
                keep(0, x, r, n, clean(pltpu.roll(inc[x, rows, :], x, 1), r, n))
        slim(lambda x, rows: cb[x, rows, :], lambda side: bslim_out, (0,))

    loaded(3)
    with scope("wait_barrier"):
        pl.semaphore_wait(barrier, len(group_a) + len(group_b) + has_out.astype(jnp.int32) + across)

    @pl.when(runs)
    def _():
        send_x(0)
        send_y(0)
        each(coef_copies, lambda c: c.start())

    late = half - 1
    d_order = [0, late] + list(range(1, late))
    third = half // 4 + 1
    d_round, d_side, d_straight = d_order[:third], d_order[third : half - third], d_order[half - third :]
    e_order = list(range(1, late)) + [0, late]
    e_round = e_order[: 2 * third : 2]

    def pair_of(ref, p):
        return ref.at[pl.ds(2 * p, 2), valid, :]

    def d_copy(p):
        to = jnp.where(t == XS, last_t, t - 1) if p in d_round else t - 1
        return rdma(pair_of(dual, p), pair_of(later, p), d_send.at[0], d_recv.at[p], tm=to)

    def d_pass(p):
        return rdma(pair_of(later, p), pair_of(later, p), d_send.at[1], d_recv.at[p], tm=XS - 1)

    def s_copy(i):
        return rdma(pair_of(dual, d_side[i]), pair_of(side, i), d_send.at[0], s_recv.at[i], tm=XS + 1)

    def s_pass(i):
        p = d_side[i]
        return rdma(pair_of(side, i), pair_of(later, p), d_send.at[1], d_recv.at[p], tm=XS - 1)

    @pl.when(t > 0)
    def _():
        for p in d_round:
            d_copy(p).start()

    @pl.when(t == XS)
    def _():
        for i in range(len(d_side)):
            s_copy(i).start()

    @pl.when((t > 0) & (t != XS))
    def _():
        for p in d_side + d_straight:
            d_copy(p).start()

    for i in range(4, 8):
        load(i)

    @pl.when(t == last_t)
    def _():
        for p in d_round:
            with scope(f"relay_d{p}"):
                wait(pair_of(later, p), d_recv.at[p])
            d_pass(p).start()

    mix_copy.wait()
    mix = jnp.concatenate([mix_r[...], jnp.zeros((L, 2 * LANES - L), F32)], axis=1)
    mix = jnp.concatenate([mix, jnp.zeros((2 * LANES - L, 2 * LANES), F32)], axis=0)
    wcat[0] = widen(mix[:R])
    wcat[1] = widen(mix.T[:R])

    def mixed(which, pair, emit):
        out = jnp.dot(wcat[which], tb[pair], preferred_element_type=F32)
        for j in range(2):
            for r, n in chunks:
                emit(2 * pair + j, r, n, out[r : r + n, j * LANES : (j + 1) * LANES])

    def put(pair, j, r, n, v):
        high = v.astype(BF16)
        low = (v - high.astype(F32)).astype(BF16)
        cols = pl.ds(j * LANES, LANES)
        tail = R - LANES
        main = min(n, LANES - r)
        if main > 0:
            tb[pair, pl.ds(r, main), cols] = high[:main]
            tb[pair, pl.ds(LANES + r, main), cols] = low[:main]
            tb[pair, pl.ds(2 * LANES + r, main), cols] = high[:main]
        if main < n:
            m = max(main, 0)
            o = 3 * LANES + r + m - LANES
            tb[pair, pl.ds(o, n - m), cols] = high[m:]
            tb[pair, pl.ds(o + tail, n - m), cols] = low[m:]
            tb[pair, pl.ds(o + 2 * tail, n - m), cols] = high[m:]

    def tangent(k, x, r, n):
        rows = pl.ds(r, n)
        v = state[k, x + 1, rows, :]
        from_low = ca[x, rows, :] * state[k, x, rows, :] + jnp.where(
            at_lane(x - 1, n), edges[0, rows, :], cb[x, rows, :] * v
        )
        from_high = state[k, x + 2, rows, :] + jnp.where(at_lane(x, n), edges[1, rows, :], v)
        return cc[x, rows, :] * v + pltpu.roll(from_low, 1, 1) + sb[rows, :] * pltpu.roll(from_high, LANES - 1, 1)

    def adjoint(k, x, r, n):
        rows = pl.ds(r, n)
        w = state[k, x + 1, rows, :]
        low = state[k, x, rows, :] + jnp.where(at_lane(x - 1, n), edges[0, rows, :], w)
        up_x = pltpu.roll(state[k, x + 2, rows, :], LANES - 1, 1)
        up_y = pltpu.roll(jnp.where(at_lane(x, n), edges[1, rows, :], w), LANES - 1, 1)
        out = cc[x, rows, :] * w + ca[x + 1, rows, :] * up_x + cb[x, rows, :] * up_y
        return out + sb[rows, :] * pltpu.roll(low, 1, 1)

    def e_copy(p):
        to = jnp.where(t == XS - 1, 0, t + 1) if p in e_round else t + 1
        return rdma(pair_of(end, p), pair_of(earlier, p), e_send.at[0], e_recv.at[p], tm=to)

    def e_pass(p):
        return rdma(pair_of(earlier, p), pair_of(earlier, p), e_send.at[1], e_recv.at[p], tm=XS)

    def keep_end(x, r, n, v):
        end[x, pl.ds(r, n), :] = pltpu.roll(v, (LANES - x) % LANES, 1)

    @pl.when(runs)
    def _():
        for k in range(STEPS):
            with scope(f"halo_y{k}"):
                if k == 0:
                    @pl.when(y > 0)
                    def _():
                        wait(bslim_in, c_recv.at[1])
                    for i in range(R // 8):
                        bhalo[pl.ds(8 * i, 8), :] = unslim(bslim_in, i)
                recv_y(k)
            for i, pair in enumerate(e_order):
                if pair == 0:
                    with scope(f"halo_x{k}"):
                        recv_x(k)
                        if k == 0:
                            @pl.when(g > 0)
                            def _():
                                wait(ca.at[0], c_recv.at[0])
                for j in range(2):
                    for r, n in chunks:
                        put(pair, j, r, n, tangent(k, 2 * pair + j, r, n))
                mixed(0, pair, functools.partial(keep, k + 1) if k < STEPS - 1 else keep_end)
                if k == STEPS - 1 and i > 0:
                    e_copy(e_order[i - 1]).start()
            if k < STEPS - 1:
                send_x(k + 1)
                send_y(k + 1)
            else:
                e_copy(e_order[-1]).start()
            if k == STEPS - 2:
                @pl.when(t == XS)
                def _():
                    for p in d_straight:
                        d_copy(p).start()

                @pl.when(t == XS + 1)
                def _():
                    for i in range(len(d_side)):
                        with scope(f"side{i}"):
                            wait(pair_of(side, i), s_recv.at[i])
                        s_pass(i).start()

    for i in range(4, 8):
        loaded(i)
    for x in range(NP):
        for r, n in chunks:
            rows = pl.ds(r, n)
            forc[x, rows, :] = forc[x, rows, :] - ev[x, rows, :] * dual[x, rows, :] - inc[x, rows, :]
            grad[x, rows, :] = grad[x, rows, :] - ob[x, rows, :] * inc[x, rows, :] - dual[x, rows, :]

    @pl.when(runs)
    def _():
        for k in range(STEPS, 2 * STEPS):
            if k > STEPS:
                with scope(f"halo_y{k}"):
                    recv_y(k - 1)
            for i, pair in enumerate(d_order if k == STEPS else e_order):
                if k == STEPS:
                    if i % 2 == 0 and i // 2 < len(e_round):
                        @pl.when(t == 0)
                        def _():
                            p = e_round[i // 2]
                            with scope(f"relay_e{p}"):
                                wait(pair_of(earlier, p), e_recv.at[p])
                            e_pass(p).start()
                    with scope(f"wait_d{pair}"):
                        wait(pair_of(later, pair), d_recv.at[pair])
                elif pair == 0:
                    with scope(f"halo_x{k}"):
                        recv_x(k - 1)
                for j in range(2):
                    x = 2 * pair + j
                    for r, n in chunks:
                        if k == STEPS:
                            v = clean(pltpu.roll(later[x, pl.ds(r, n), :], x, 1), r, n)
                        else:
                            v = adjoint(k - 1, x, r, n)
                        put(pair, j, r, n, v)
                mixed(1, pair, functools.partial(keep, k))
                if k == STEPS and i == 1:
                    send_x(k)
            if k > STEPS:
                send_x(k)
            send_y(k)

    def squared(v, r, n):
        v = clean(v, r, n)
        return jnp.sum((v * v).reshape(n // 8, 8, LANES), axis=0)

    def add_earlier():
        total = acc[...]
        for p in e_order:
            with scope(f"wait_e{p}"):
                wait(pair_of(earlier, p), e_recv.at[p])
            for x in (2 * p, 2 * p + 1):
                for r, n in chunks:
                    rows = pl.ds(r, n)
                    v = forc[x, rows, :] + earlier[x, rows, :]
                    forc[x, rows, :] = v
                    total = total + squared(v, r, n)
        acc[...] = total

    acc[...] = jnp.zeros((8, LANES), F32)

    @pl.when((t > 0) & (t != XS))
    def _():
        add_earlier()

    @pl.when(runs)
    def _():
        k = 2 * STEPS - 1
        with scope("halo_last"):
            recv_y(k)
            recv_x(k)
        total = acc[...]
        for x in range(NP):
            for r, n in chunks:
                rows = pl.ds(r, n)
                back = adjoint(k, x, r, n)
                v = grad[x, rows, :] + pltpu.roll(back, (LANES - x) % LANES, 1)
                grad[x, rows, :] = v
                total = total + squared(v, r, n)
        acc[...] = total

    @pl.when(t == XS)
    def _():
        add_earlier()

    for on, ref in ((t == 0, forc), (t == last_t, grad)):
        @pl.when(on)
        def _():
            total = acc[...]
            for x in range(NP):
                for r, n in chunks:
                    total = total + squared(ref[x, pl.ds(r, n), :], r, n)
            acc[...] = total

    stage_a[0] = jnp.sum(acc[...], axis=0, keepdims=True)
    for i, p in enumerate(group_a):
        rdma(stage_a.at[0], stage_a.at[i + 1], p_send.at[0], p_recv.at[0], **peer_a(*p)).start()
    everyone = stage_a.at[pl.ds(1, len(group_a))]
    with scope("sum_a"):
        wait(everyone, p_recv.at[0])
    stage_b[0] = jnp.sum(stage_a[...], axis=0)
    for i, p in enumerate(group_b):
        rdma(stage_b.at[0], stage_b.at[i + 1], p_send.at[1], p_recv.at[1], **peer_b(*p)).start()
    everyone_b = stage_b.at[pl.ds(1, len(group_b))]

    wait(everyone, p_send.at[0])

    @pl.when(runs)
    def _():
        for k in range(2 * STEPS):
            each(halo_copies(k), lambda c: c.wait_send())
        each(coef_copies, lambda c: c.wait_send())
        wait(end.at[:, valid, :], e_send.at[0])

    @pl.when(t > 0)
    def _():
        wait(dual.at[:, valid, :], d_send.at[0])

    @pl.when(t == last_t)
    def _():
        wait(later.at[pl.ds(0, 2 * len(d_round)), valid, :], d_send.at[1])

    @pl.when(t == XS + 1)
    def _():
        wait(side.at[pl.ds(0, 2 * len(d_side)), valid, :], d_send.at[1])

    @pl.when(t == 0)
    def _():
        wait(later.at[pl.ds(0, 2 * len(e_round)), valid, :], e_send.at[1])

    with scope("sum_b"):
        wait(everyone_b, p_recv.at[1])
    sums[...] = jnp.sum(stage_b[...], axis=0)
    wait(everyone_b, p_send.at[1])


def finish(sz, forc, grad, dual, inc, sums, out_dual, out_incr, done, sem):
    chunks = [(r, min(48, sz.rows - r)) for r in range(0, sz.rows, 48)]
    valid = pl.ds(0, sz.levels)
    global_sum = jnp.sum(sums[...], keepdims=True)
    count = 2 * sz.levels * sz.planes * LANES * sz.tm * sz.gx * sz.gy
    root_mean = jnp.sqrt(global_sum / count + 1e-06)
    scale = jnp.minimum(1.0, 0.5 / root_mean)
    outs = (out_dual, out_incr)
    for x in range(sz.planes):
        for i, (base, step) in enumerate(((dual, forc), (inc, grad))):
            for r, n in chunks:
                rows = pl.ds(r, n)
                done[i, x, rows, :] = base[x, rows, :] + scale * step[x, rows, :]
            pltpu.make_async_copy(done.at[i, x, valid, :], outs[i].at[0, :, x, :], sem.at[i]).start()
    for i in range(2):
        whole = done.at[i, :, valid, :]
        pltpu.make_async_copy(whole, whole, sem.at[i]).wait()


def solution(mesh):
    def local(increment, dual_state, forcing, gradient, courant_x, courant_y, error_var, obs_weight, diffusion, level_mix):
        _, levels, planes, lanes = increment.shape
        assert lanes == LANES
        sz = Sizes(mesh, levels, planes)
        R = sz.rows
        field = pltpu.VMEM((planes, R, LANES), F32)
        plane = pltpu.VMEM((R, LANES), F32)
        n = 2 * STEPS
        thin = 8 * -(-R * planes // (8 * LANES))
        slim = pltpu.VMEM((thin, LANES), F32)
        dma = pltpu.SemaphoreType.DMA
        any_spec = pl.BlockSpec(memory_space=pltpu.HBM)
        vmem_spec = pl.BlockSpec(memory_space=pltpu.VMEM)
        block = jax.ShapeDtypeStruct(increment.shape, F32)
        kept = pl.pallas_call(
            functools.partial(kernel, sz),
            name="saddle",
            out_shape=[pltpu.VMEM((planes, R, LANES), F32)] * 4 + [pltpu.VMEM((1, LANES), F32)],
            in_specs=[any_spec] * 10,
            out_specs=[pl.BlockSpec(memory_space=pltpu.VMEM)] * 5,
            scratch_shapes=[field] * 7
            + [
                pltpu.VMEM((planes // 2, R, LANES), F32),
                pltpu.VMEM((8, LANES), F32),
                pltpu.VMEM((planes + 1, R, LANES), F32),
                field,
                field,
                plane,
                pltpu.VMEM((n, planes + 2, R, LANES), F32),
                pltpu.VMEM((n, 2, thin, LANES), F32),
                pltpu.VMEM((n, 2, thin, LANES), F32),
                pltpu.VMEM((2, R, LANES), F32),
                pltpu.VMEM((n, 2, R, LANES), F32),
                slim,
                slim,
                plane,
                plane,
                pltpu.VMEM((1, levels), F32),
                pltpu.VMEM((levels, levels), F32),
                pltpu.VMEM((2, R, sz.depth), BF16),
                pltpu.VMEM((planes // 2, sz.depth, 2 * LANES), BF16),
                pltpu.VMEM((sz.xs * sz.gy * 2, 1, LANES), F32),
                pltpu.VMEM((sz.gx, 1, LANES), F32),
                dma((10,)),
                dma((2,)),
                dma((planes // 2,)),
                dma((planes // 2,)),
                dma((2,)),
                dma((planes // 2,)),
                dma((n, 4)),
                dma((n, 4)),
                dma((2,)),
                dma((2,)),
                dma((2,)),
                dma((2,)),
            ],
            compiler_params=pltpu.CompilerParams(
                collective_id=0, has_side_effects=True, vmem_limit_bytes=60_000_000
            ),
        )(
            increment, dual_state, forcing, gradient, courant_x, courant_y, error_var, obs_weight,
            diffusion.reshape(1, -1), level_mix,
        )
        return pl.pallas_call(
            functools.partial(finish, sz),
            name="finish",
            out_shape=[block, block],
            in_specs=[vmem_spec] * 5,
            out_specs=[any_spec] * 2,
            scratch_shapes=[pltpu.VMEM((2, planes, R, LANES), F32), dma((2,))],
            compiler_params=pltpu.CompilerParams(vmem_limit_bytes=6_000_000),
        )(*kept)

    spec = P("tm", None, "gx", "gy")
    return jax.shard_map(
        local,
        mesh=mesh,
        in_specs=(spec,) * 8 + (P(), P()),
        out_specs=(spec, spec),
        check_vma=False,
    )
```

time: 88.6 us -> 79.7 us (0.90)
  Pallas kernels: 84 us -> 78.8 us
  local copies, waits for them, and re-layouts: 3.41 us -> 0 us
    pallas_call x1 -> x2, Pallas kernels: 84 us -> 78.8 us  [the longest x1 77.3 us: local(): pl.pallas_call(functools.partial(kernel, sz), name='saddle', out_shape=[p...]
    unnamed x4 -> x0, local copies, waits for them, and re-layouts: 3.41 us -> none
where the time goes in v1:
time: 79.7 us; the launch traced here: 79.6 us
  Pallas kernels  78.8 us (99%)
  between operations  0.8 us (1%)
    pallas_call x1, Pallas kernels, local(): pl.pallas_call(functools.partial(kernel, sz), name='saddle', out_shape=[p...  77.3 us

profile of v1, /device:TPU:1, one launch (start us, length us, event | category | flops | bytes accessed | tf_op | source)
XLA Modules:
  0.0 79.6 jit_solution(10191949433889972260)
XLA Ops:
  0.6 77.3 %saddle.1 = (f32[16,144,128]{2,1,0:T(8,128)S(1)}, f32[16,144,128]{2,1,0:T(8,128)S(1)}, f32[16,144,128]{2,1,0:T(8,128)S(1)}, f32[16,144,128]{2,1,0:T(8,128)S(1)}, f32[1,128]{1,0:T(1,128)S(1)}) custom-call(f32[1,137,16,128]{3,2,1,0:T(8,128)} %inc_h.1, f32[1,137,16,128]{3,2,1,0:T(8,128)} %dual_h.1, f32[1,137,16,128]{3,2,1,0:T(8,128)} %forc_h.1, ...), custom_call_target="tpu_custom_call" | custom-call | tf_op jit(solution)/shard_map/saddle/pallas_call | solution.py:588
  77.9 1.5 %finish.1 = (f32[1,137,16,128]{3,2,1,0:T(8,128)}, f32[1,137,16,128]{3,2,1,0:T(8,128)}) custom-call(f32[16,144,128]{2,1,0:T(8,128)S(1)} %get-tuple-element.7.forc, f32[16,144,128]{2,1,0:T(8,128)S(1)} %get-tuple-element.8.grad, f32[16,144,128]{2,1,0:T(8,128)S(1)} %get-tuple-element.9.dual, f32[16,144,128]{2,1,0:T(8,128)S(1)} %get-tuple-element.10.inc, ...), custom_call_target="tpu_custom_call" | custom-call | tf_op jit(solution)/shard_map/finish/pallas_call | solution.py:637

commit v2 on v1

--- a/solution.py
+++ b/solution.py
@@ -42,6 +42,7 @@
     last_t = sz.tm - 1
     zchips = sz.gx // 2
     half = NP // 2
+    helper = XS + 2
     scope = jax.named_scope
 
     def rdma(src, dst, ssem, rsem, **where):
@@ -80,14 +81,19 @@
     def _():
         greet({"gx": outward})
 
-    across = jnp.where(t == XS - 1, 2, jnp.where((t == XS) | (t == XS + 1), 1, 0))
+    other = zl * 2 + 1 - core
+    across = jnp.where((t == XS - 1) | (t == XS), 2, jnp.where((t == 0) | (t == helper), 1, 0))
+
+    @pl.when((t == 0) | (t == XS))
+    def _():
+        greet({"tm": XS - t, "gx": other})
 
     @pl.when(t == XS - 1)
     def _():
         greet({"tm": XS})
-        greet({"tm": XS + 1})
-
-    @pl.when((t == XS) | (t == XS + 1))
+        greet({"tm": helper})
+
+    @pl.when((t == XS) | (t == helper))
     def _():
         greet({"tm": XS - 1})
 
@@ -268,9 +274,10 @@
     late = half - 1
     d_order = [0, late] + list(range(1, late))
     third = half // 4 + 1
-    d_round, d_side, d_straight = d_order[:third], d_order[third : half - third], d_order[half - third :]
+    d_round, d_side, d_straight = d_order[:third], d_order[third : 2 * third], d_order[2 * third :]
     e_order = list(range(1, late)) + [0, late]
-    e_round = e_order[: 2 * third : 2]
+    straight = core == lax.rem(zl, 2)
+    around = (t == XS - 1) & jnp.logical_not(straight)
 
     def pair_of(ref, p):
         return ref.at[pl.ds(2 * p, 2), valid, :]
@@ -283,7 +290,7 @@
         return rdma(pair_of(later, p), pair_of(later, p), d_send.at[1], d_recv.at[p], tm=XS - 1)
 
     def s_copy(i):
-        return rdma(pair_of(dual, d_side[i]), pair_of(side, i), d_send.at[0], s_recv.at[i], tm=XS + 1)
+        return rdma(pair_of(dual, d_side[i]), pair_of(side, i), d_send.at[0], s_recv.at[i], tm=helper)
 
     def s_pass(i):
         p = d_side[i]
@@ -362,11 +369,11 @@
         return out + sb[rows, :] * pltpu.roll(low, 1, 1)
 
     def e_copy(p):
-        to = jnp.where(t == XS - 1, 0, t + 1) if p in e_round else t + 1
-        return rdma(pair_of(end, p), pair_of(earlier, p), e_send.at[0], e_recv.at[p], tm=to)
+        to, column = jnp.where(around, 0, t + 1), jnp.where(around, other, g)
+        return rdma(pair_of(end, p), pair_of(earlier, p), e_send.at[0], e_recv.at[p], tm=to, gx=column)
 
     def e_pass(p):
-        return rdma(pair_of(earlier, p), pair_of(earlier, p), e_send.at[1], e_recv.at[p], tm=XS)
+        return rdma(pair_of(earlier, p), pair_of(earlier, p), e_send.at[1], e_recv.at[p], tm=XS, gx=other)
 
     def keep_end(x, r, n, v):
         end[x, pl.ds(r, n), :] = pltpu.roll(v, (LANES - x) % LANES, 1)
@@ -394,20 +401,22 @@
                     for r, n in chunks:
                         put(pair, j, r, n, tangent(k, 2 * pair + j, r, n))
                 mixed(0, pair, functools.partial(keep, k + 1) if k < STEPS - 1 else keep_end)
-                if k == STEPS - 1 and i > 0:
-                    e_copy(e_order[i - 1]).start()
+                if k == STEPS - 1 and i == 2:
+                    for p in e_order[:i]:
+                        e_copy(p).start()
             if k < STEPS - 1:
                 send_x(k + 1)
                 send_y(k + 1)
             else:
-                e_copy(e_order[-1]).start()
+                for p in e_order[2:]:
+                    e_copy(p).start()
             if k == STEPS - 2:
                 @pl.when(t == XS)
                 def _():
                     for p in d_straight:
                         d_copy(p).start()
 
-                @pl.when(t == XS + 1)
+                @pl.when(t == helper)
                 def _():
                     for i in range(len(d_side)):
                         with scope(f"side{i}"):
@@ -430,13 +439,12 @@
                     recv_y(k - 1)
             for i, pair in enumerate(d_order if k == STEPS else e_order):
                 if k == STEPS:
-                    if i % 2 == 0 and i // 2 < len(e_round):
-                        @pl.when(t == 0)
-                        def _():
-                            p = e_round[i // 2]
-                            with scope(f"relay_e{p}"):
-                                wait(pair_of(earlier, p), e_recv.at[p])
-                            e_pass(p).start()
+                    @pl.when((t == 0) & straight)
+                    def _():
+                        p = e_order[i]
+                        with scope(f"relay_e{p}"):
+                            wait(pair_of(earlier, p), e_recv.at[p])
+                        e_pass(p).start()
                     with scope(f"wait_d{pair}"):
                         wait(pair_of(later, pair), d_recv.at[pair])
                 elif pair == 0:
@@ -537,13 +545,13 @@
     def _():
         wait(later.at[pl.ds(0, 2 * len(d_round)), valid, :], d_send.at[1])
 
-    @pl.when(t == XS + 1)
+    @pl.when(t == helper)
     def _():
         wait(side.at[pl.ds(0, 2 * len(d_side)), valid, :], d_send.at[1])
 
-    @pl.when(t == 0)
-    def _():
-        wait(later.at[pl.ds(0, 2 * len(e_round)), valid, :], e_send.at[1])
+    @pl.when((t == 0) & straight)
+    def _():
+        wait(earlier.at[:, valid, :], e_send.at[1])
 
     with scope("sum_b"):
         wait(everyone_b, p_recv.at[1])

time: 79.7 us -> 71.4 us (0.90)
  Pallas kernels: 78.8 us -> 70.5 us
    pallas_call x1, Pallas kernels: 77.3 us -> 69 us  [local(): pl.pallas_call(functools.partial(kernel, sz), name='saddle', out_shape=[p...]
where the time goes in v2:
time: 71.4 us; the launch traced here: 71.3 us
  Pallas kernels  70.5 us (99%)
  between operations  0.8 us (1%)
    pallas_call x1, Pallas kernels, local(): pl.pallas_call(functools.partial(kernel, sz), name='saddle', out_shape=[p...  69 us
    pallas_call x1, Pallas kernels, local(): pl.pallas_call(functools.partial(finish, sz), name='finish', out_shape=[b...  1.49 us

profile of v2, /device:TPU:1, one launch (start us, length us, event | category | flops | bytes accessed | tf_op | source)
XLA Modules:
  0.0 71.3 jit_solution(16326763904385734192)
XLA Ops:
  0.6 69.0 %saddle.1 = (f32[16,144,128]{2,1,0:T(8,128)S(1)}, f32[16,144,128]{2,1,0:T(8,128)S(1)}, f32[16,144,128]{2,1,0:T(8,128)S(1)}, f32[16,144,128]{2,1,0:T(8,128)S(1)}, f32[1,128]{1,0:T(1,128)S(1)}) custom-call(f32[1,137,16,128]{3,2,1,0:T(8,128)} %inc_h.1, f32[1,137,16,128]{3,2,1,0:T(8,128)} %dual_h.1, f32[1,137,16,128]{3,2,1,0:T(8,128)} %forc_h.1, ...), custom_call_target="tpu_custom_call" | custom-call | tf_op jit(solution)/shard_map/saddle/pallas_call | solution.py:596
  69.7 1.5 %finish.1 = (f32[1,137,16,128]{3,2,1,0:T(8,128)}, f32[1,137,16,128]{3,2,1,0:T(8,128)}) custom-call(f32[16,144,128]{2,1,0:T(8,128)S(1)} %get-tuple-element.7.forc, f32[16,144,128]{2,1,0:T(8,128)S(1)} %get-tuple-element.8.grad, f32[16,144,128]{2,1,0:T(8,128)S(1)} %get-tuple-element.9.dual, f32[16,144,128]{2,1,0:T(8,128)S(1)} %get-tuple-element.10.inc, ...), custom_call_target="tpu_custom_call" | custom-call | tf_op jit(solution)/shard_map/finish/pallas_call | solution.py:645

commit v3 on v2

--- a/solution.py
+++ b/solution.py
@@ -29,7 +29,7 @@
     inc_h, dual_h, forc_h, grad_h, cx_h, cy_h, ev_h, ob_h, diff_h, mix_h,
     forc, grad, dual, inc, sums,
     cx, cy, ev, ob,
-    later, earlier, end, side, acc,
+    later, earlier, end, side, acc, cols, zed, bown,
     ca, cb, cc, sb, state, slim_out, slim_in, edges, xsend, bslim_out, bslim_in, bhalo, asend,
     diff_r, mix_r, wcat, tb, stage_a, stage_b,
     load_sem, d_send, d_recv, s_recv, e_send, e_recv, h_send, h_recv, c_send, c_recv, p_send, p_recv,
@@ -166,25 +166,24 @@
 
     share = LANES // NP
 
+    def slim_tiles(tile, dst, e):
+        for o in range(0, R // 8, share):
+            acc = tile(pl.ds(8 * o, 8))
+            for j in range(1, min(share, R // 8 - o)):
+                turned = pltpu.roll(tile(pl.ds(8 * (o + j), 8)), NP * j, 1)
+                inside = (lane >= NP * j + e - 1) & (lane < NP * (j + 1) + e - 1)
+                acc = jnp.where(inside, turned, acc)
+            dst[pl.ds(8 * (o // share), 8), :] = acc
+
     def slim(planes, dst, sides):
-        for o in range(0, R // 8, share):
-            acc = {}
-            for j in range(min(share, R // 8 - o)):
-                rows = pl.ds(8 * (o + j), 8)
-                part = {}
-                for x in range(NP):
-                    v = planes(x, rows)
-                    for side in sides:
-                        part[side] = jnp.where(lane == (x + side - 1) % LANES, v, part[side]) if x else v
-                for side in sides:
-                    if j:
-                        turned = pltpu.roll(part[side], NP * j, 1)
-                        inside = (lane >= NP * j + side - 1) & (lane < NP * (j + 1) + side - 1)
-                        acc[side] = jnp.where(inside, turned, acc[side])
-                    else:
-                        acc[side] = part[side]
-            for side in sides:
-                dst(side)[pl.ds(8 * (o // share), 8), :] = acc[side]
+        for e in sides:
+            def tile(rows):
+                part = planes(0, rows)
+                for x in range(1, NP):
+                    part = jnp.where(lane == x + e - 1, planes(x, rows), part)
+                return part
+
+            slim_tiles(tile, dst(e), e)
 
     def unslim(src, i):
         tile = src[pl.ds(8 * (i // share), 8), :]
@@ -242,24 +241,32 @@
         (y < sz.gy - 1, bslim_out, bslim_in, c_send.at[1], c_recv.at[1], {"gy": y + 1}),
     )
     runs = t != last_t
-    for i in range(3):
-        loaded(i)
+    def turned_field(ref, x, r, n):
+        return pltpu.roll(ref[x, pl.ds(r, n), :], x, 1)
+
+    loaded(0)
+
+    @pl.when(runs)
+    def _():
+        for x in range(NP):
+            for r, n in chunks:
+                keep(0, x, r, n, clean(turned_field(inc, x, r, n), r, n))
+        slim(lambda x, rows: state[0, x + 1, rows, :], lambda side: slim_out.at[0, side], (0, 1))
+
+    loaded(1)
+    loaded(2)
 
     @pl.when(runs)
     def _():
         for x in range(NP):
             for r, n in chunks:
                 rows = pl.ds(r, n)
-                s = sb[rows, :]
-                a = clean(pltpu.roll(cx[x, rows, :], x, 1) + s, r, n)
-                b = clean(pltpu.roll(cy[x, rows, :], x, 1) + s, r, n)
-                ca[x + 1, rows, :] = a
-                cb[x, rows, :] = b
-                cc[x, rows, :] = 1.0 - 2.0 * s - a - b
-                if x == NP - 1:
-                    asend[rows, :] = pltpu.roll(a, LANES - NP, 1)
-                keep(0, x, r, n, clean(pltpu.roll(inc[x, rows, :], x, 1), r, n))
+                cb[x, rows, :] = clean(turned_field(cy, x, r, n) + sb[rows, :], r, n)
         slim(lambda x, rows: cb[x, rows, :], lambda side: bslim_out, (0,))
+        for r, n in chunks:
+            rows = pl.ds(r, n)
+            a = clean(turned_field(cx, NP - 1, r, n) + sb[rows, :], r, n)
+            asend[rows, :] = pltpu.roll(a, LANES - NP, 1)
 
     loaded(3)
     with scope("wait_barrier"):
@@ -268,7 +275,7 @@
     @pl.when(runs)
     def _():
         send_x(0)
-        send_y(0)
+        each(halo_copies(0)[2:], lambda c: c.start())
         each(coef_copies, lambda c: c.start())
 
     late = half - 1
@@ -320,6 +327,16 @@
             with scope(f"relay_d{p}"):
                 wait(pair_of(later, p), d_recv.at[p])
             d_pass(p).start()
+
+    @pl.when(runs)
+    def _():
+        for x in range(NP):
+            for r, n in chunks:
+                rows = pl.ds(r, n)
+                s = sb[rows, :]
+                a = clean(turned_field(cx, x, r, n) + s, r, n)
+                ca[x + 1, rows, :] = a
+                cc[x, rows, :] = 1.0 - 2.0 * s - a - cb[x, rows, :]
 
     mix_copy.wait()
     mix = jnp.concatenate([mix_r[...], jnp.zeros((L, 2 * LANES - L), F32)], axis=1)
@@ -350,23 +367,94 @@
             tb[pair, pl.ds(o + tail, n - m), cols] = low[m:]
             tb[pair, pl.ds(o + 2 * tail, n - m), cols] = high[m:]
 
-    def tangent(k, x, r, n):
+    def edge_of(side, rows, edge):
+        return edges[side, rows, :] if edge else 0.0
+
+    def tangent(k, x, r, n, edge=True):
         rows = pl.ds(r, n)
         v = state[k, x + 1, rows, :]
         from_low = ca[x, rows, :] * state[k, x, rows, :] + jnp.where(
-            at_lane(x - 1, n), edges[0, rows, :], cb[x, rows, :] * v
+            at_lane(x - 1, n), edge_of(0, rows, edge), cb[x, rows, :] * v
         )
-        from_high = state[k, x + 2, rows, :] + jnp.where(at_lane(x, n), edges[1, rows, :], v)
+        from_high = state[k, x + 2, rows, :] + jnp.where(at_lane(x, n), edge_of(1, rows, edge), v)
         return cc[x, rows, :] * v + pltpu.roll(from_low, 1, 1) + sb[rows, :] * pltpu.roll(from_high, LANES - 1, 1)
 
-    def adjoint(k, x, r, n):
+    def adjoint(k, x, r, n, edge=True):
         rows = pl.ds(r, n)
         w = state[k, x + 1, rows, :]
-        low = state[k, x, rows, :] + jnp.where(at_lane(x - 1, n), edges[0, rows, :], w)
+        low = state[k, x, rows, :] + jnp.where(at_lane(x - 1, n), edge_of(0, rows, edge), w)
         up_x = pltpu.roll(state[k, x + 2, rows, :], LANES - 1, 1)
-        up_y = pltpu.roll(jnp.where(at_lane(x, n), edges[1, rows, :], w), LANES - 1, 1)
+        up_y = pltpu.roll(jnp.where(at_lane(x, n), edge_of(1, rows, edge), w), LANES - 1, 1)
         out = cc[x, rows, :] * w + ca[x + 1, rows, :] * up_x + cb[x, rows, :] * up_y
         return out + sb[rows, :] * pltpu.roll(low, 1, 1)
+
+    def tangent_edges(rows):
+        first = pltpu.roll(edges[0, rows, :], 1, 1)
+        return first, sb[rows, :] * pltpu.roll(edges[1, rows, :], LANES - 1, 1)
+
+    def adjoint_edges(rows):
+        first = sb[rows, :] * pltpu.roll(edges[0, rows, :], 1, 1)
+        return first, bown[rows, :] * pltpu.roll(edges[1, rows, :], LANES - 1, 1)
+
+    inner_pairs, outer_pairs = list(range(1, half - 1)), [0, half - 1]
+    inner = list(range(2, NP - 2))
+    outer = [0, 1, NP - 2, NP - 1]
+
+    def step_inner(k, which, stencil, emit):
+        for pair in inner_pairs:
+            for j in range(2):
+                for r, n in chunks:
+                    put(pair, j, r, n, stencil(k, 2 * pair + j, r, n, False))
+            mixed(which, pair, emit)
+
+    def step_edges(which, stencil_edges):
+        for r, n in chunks:
+            for j, v in enumerate(stencil_edges(pl.ds(r, n))):
+                put(half, j, r, n, v)
+        zed[...] = jnp.dot(wcat[which], tb[half], preferred_element_type=F32)
+
+    def step_outer(k, which, stencil, emit):
+        for pair in outer_pairs:
+            for j in range(2):
+                for r, n in chunks:
+                    put(pair, j, r, n, stencil(k, 2 * pair + j, r, n))
+            mixed(which, pair, emit)
+
+    def advance(k, which, stencil, stencil_edges, extra_y, extra_x, after):
+        emit = functools.partial(keep, k + 1)
+        step_inner(k, which, stencil, emit)
+        for i in range(R // 8):
+            rows = pl.ds(8 * i, 8)
+            part = [None, None]
+            for x in inner:
+                v = state[k + 1, x + 1, rows, :]
+                for e in range(2):
+                    part[e] = v if part[e] is None else jnp.where(lane == x + e - 1, v, part[e])
+            for e in range(2):
+                cols[e, rows, :] = part[e]
+        with scope(f"halo_y{k}"):
+            extra_y()
+            recv_y(k)
+        step_edges(which, stencil_edges)
+        with scope(f"halo_x{k}"):
+            extra_x()
+            recv_x(k)
+        step_outer(k, which, stencil, emit)
+        send_x(k + 1)
+        for i in range(R // 8):
+            rows = pl.ds(8 * i, 8)
+            for e in range(2):
+                v = cols[e, rows, :] + zed[rows, pl.ds((1 - e) * LANES, LANES)]
+                for x in outer:
+                    v = jnp.where(lane == (x + e - 1) % LANES, state[k + 1, x + 1, rows, :], v)
+                cols[e, rows, :] = v
+        for e in range(2):
+            slim_tiles(lambda rows: cols[e, rows, :], slim_out.at[k + 1, e], e)
+        each(halo_copies(k + 1)[2:], lambda c: c.start())
+        after()
+        for x in inner:
+            for e in range(2):
+                pltpu.store(state.at[k + 1, x + 1], cols[e], mask=at_lane(x + e - 1, R))
 
     def e_copy(p):
         to, column = jnp.where(around, 0, t + 1), jnp.where(around, other, g)
@@ -378,50 +466,67 @@
     def keep_end(x, r, n, v):
         end[x, pl.ds(r, n), :] = pltpu.roll(v, (LANES - x) % LANES, 1)
 
+    def nothing():
+        pass
+
+    def first_y():
+        @pl.when(y > 0)
+        def _():
+            wait(bslim_in, c_recv.at[1])
+        for i in range(R // 8):
+            bhalo[pl.ds(8 * i, 8), :] = unslim(bslim_in, i)
+
+    def first_x():
+        @pl.when(g > 0)
+        def _():
+            wait(ca.at[0], c_recv.at[0])
+
+    def cross():
+        @pl.when(t == XS)
+        def _():
+            for p in d_straight:
+                d_copy(p).start()
+
+        @pl.when(t == helper)
+        def _():
+            for i in range(len(d_side)):
+                with scope(f"side{i}"):
+                    wait(pair_of(side, i), s_recv.at[i])
+                s_pass(i).start()
+
+    def keep_turned(x, r, n, v):
+        end[x, pl.ds(r, n), :] = v
+
     @pl.when(runs)
     def _():
-        for k in range(STEPS):
-            with scope(f"halo_y{k}"):
-                if k == 0:
-                    @pl.when(y > 0)
-                    def _():
-                        wait(bslim_in, c_recv.at[1])
-                    for i in range(R // 8):
-                        bhalo[pl.ds(8 * i, 8), :] = unslim(bslim_in, i)
-                recv_y(k)
-            for i, pair in enumerate(e_order):
-                if pair == 0:
-                    with scope(f"halo_x{k}"):
-                        recv_x(k)
-                        if k == 0:
-                            @pl.when(g > 0)
-                            def _():
-                                wait(ca.at[0], c_recv.at[0])
-                for j in range(2):
-                    for r, n in chunks:
-                        put(pair, j, r, n, tangent(k, 2 * pair + j, r, n))
-                mixed(0, pair, functools.partial(keep, k + 1) if k < STEPS - 1 else keep_end)
-                if k == STEPS - 1 and i == 2:
-                    for p in e_order[:i]:
-                        e_copy(p).start()
-            if k < STEPS - 1:
-                send_x(k + 1)
-                send_y(k + 1)
-            else:
-                for p in e_order[2:]:
+        for k in range(STEPS - 1):
+            advance(
+                k, 0, tangent, tangent_edges,
+                nothing if k else first_y, nothing if k else first_x, cross if k == STEPS - 2 else nothing,
+            )
+        k = STEPS - 1
+        step_inner(k, 0, tangent, keep_turned)
+        for i in range(R // 8):
+            bown[pl.ds(8 * i, 8), :] = unslim(bslim_out, i)
+        with scope(f"halo_y{k}"):
+            recv_y(k)
+        step_edges(0, tangent_edges)
+        for i, pair in enumerate(inner_pairs):
+            for x in (2 * pair, 2 * pair + 1):
+                for r, n in chunks:
+                    rows = pl.ds(r, n)
+                    v = end[x, rows, :]
+                    v = jnp.where(at_lane(x, n), v + zed[rows, pl.ds(0, LANES)], v)
+                    v = jnp.where(at_lane(x - 1, n), v + zed[rows, pl.ds(LANES, LANES)], v)
+                    keep_end(x, r, n, v)
+            if i == 1:
+                for p in e_order[:2]:
                     e_copy(p).start()
-            if k == STEPS - 2:
-                @pl.when(t == XS)
-                def _():
-                    for p in d_straight:
-                        d_copy(p).start()
-
-                @pl.when(t == helper)
-                def _():
-                    for i in range(len(d_side)):
-                        with scope(f"side{i}"):
-                            wait(pair_of(side, i), s_recv.at[i])
-                        s_pass(i).start()
+        with scope(f"halo_x{k}"):
+            recv_x(k)
+        step_outer(k, 0, tangent, keep_end)
+        for p in e_order[2:]:
+            e_copy(p).start()
 
     for i in range(4, 8):
         loaded(i)
@@ -433,37 +538,30 @@
 
     @pl.when(runs)
     def _():
-        for k in range(STEPS, 2 * STEPS):
-            if k > STEPS:
-                with scope(f"halo_y{k}"):
-                    recv_y(k - 1)
-            for i, pair in enumerate(d_order if k == STEPS else e_order):
-                if k == STEPS:
-                    @pl.when((t == 0) & straight)
-                    def _():
-                        p = e_order[i]
-                        with scope(f"relay_e{p}"):
-                            wait(pair_of(earlier, p), e_recv.at[p])
-                        e_pass(p).start()
-                    with scope(f"wait_d{pair}"):
-                        wait(pair_of(later, pair), d_recv.at[pair])
-                elif pair == 0:
-                    with scope(f"halo_x{k}"):
-                        recv_x(k - 1)
-                for j in range(2):
-                    x = 2 * pair + j
-                    for r, n in chunks:
-                        if k == STEPS:
-                            v = clean(pltpu.roll(later[x, pl.ds(r, n), :], x, 1), r, n)
-                        else:
-                            v = adjoint(k - 1, x, r, n)
-                        put(pair, j, r, n, v)
-                mixed(1, pair, functools.partial(keep, k))
-                if k == STEPS and i == 1:
-                    send_x(k)
-            if k > STEPS:
+        k = STEPS
+        for i, pair in enumerate(d_order):
+            @pl.when((t == 0) & straight)
+            def _():
+                p = e_order[i]
+                with scope(f"relay_e{p}"):
+                    wait(pair_of(earlier, p), e_recv.at[p])
+                e_pass(p).start()
+
+            with scope(f"wait_d{pair}"):
+                wait(pair_of(later, pair), d_recv.at[pair])
+            for j in range(2):
+                x = 2 * pair + j
+                for r, n in chunks:
+                    put(pair, j, r, n, clean(turned_field(later, x, r, n), r, n))
+            mixed(1, pair, functools.partial(keep, k))
+            if i == 1:
                 send_x(k)
-            send_y(k)
+        send_y(k)
+        for k in range(STEPS, 2 * STEPS - 1):
+            advance(k, 1, adjoint, adjoint_edges, nothing, nothing, nothing)
+        for x in inner:
+            for r, n in chunks:
+                state[0, x + 1, pl.ds(r, n), :] = adjoint(2 * STEPS - 1, x, r, n, False)
 
     def squared(v, r, n):
         v = clean(v, r, n)
@@ -484,7 +582,7 @@
 
     acc[...] = jnp.zeros((8, LANES), F32)
 
-    @pl.when((t > 0) & (t != XS))
+    @pl.when((t > 0) & (t != XS - 1) & (t != XS))
     def _():
         add_earlier()
 
@@ -493,18 +591,30 @@
         k = 2 * STEPS - 1
         with scope("halo_last"):
             recv_y(k)
-            recv_x(k)
         total = acc[...]
-        for x in range(NP):
+        for r, n in chunks:
+            rows = pl.ds(r, n)
+            first, last = adjoint_edges(rows)
+            zed[rows, pl.ds(0, LANES)] = first
+            zed[rows, pl.ds(LANES, LANES)] = last
+        for x in inner + outer:
+            if x == outer[0]:
+                with scope("halo_last_x"):
+                    recv_x(k)
             for r, n in chunks:
                 rows = pl.ds(r, n)
-                back = adjoint(k, x, r, n)
+                if x in inner:
+                    back = state[0, x + 1, rows, :]
+                    back = jnp.where(at_lane(x, n), back + zed[rows, pl.ds(0, LANES)], back)
+                    back = jnp.where(at_lane(x - 1, n), back + zed[rows, pl.ds(LANES, LANES)], back)
+                else:
+                    back = adjoint(k, x, r, n)
                 v = grad[x, rows, :] + pltpu.roll(back, (LANES - x) % LANES, 1)
                 grad[x, rows, :] = v
                 total = total + squared(v, r, n)
         acc[...] = total
 
-    @pl.when(t == XS)
+    @pl.when((t == XS - 1) | (t == XS))
     def _():
         add_earlier()
 
@@ -603,6 +713,9 @@
             + [
                 pltpu.VMEM((planes // 2, R, LANES), F32),
                 pltpu.VMEM((8, LANES), F32),
+                pltpu.VMEM((2, R, LANES), F32),
+                pltpu.VMEM((R, 2 * LANES), F32),
+                plane,
                 pltpu.VMEM((planes + 1, R, LANES), F32),
                 field,
                 field,
@@ -619,7 +732,7 @@
                 pltpu.VMEM((1, levels), F32),
                 pltpu.VMEM((levels, levels), F32),
                 pltpu.VMEM((2, R, sz.depth), BF16),
-                pltpu.VMEM((planes // 2, sz.depth, 2 * LANES), BF16),
+                pltpu.VMEM((planes // 2 + 1, sz.depth, 2 * LANES), BF16),
                 pltpu.VMEM((sz.xs * sz.gy * 2, 1, LANES), F32),
                 pltpu.VMEM((sz.gx, 1, LANES), F32),
                 dma((10,)),

time: 71.4 us -> 66.3 us (0.929)
  Pallas kernels: 70.5 us -> 65.3 us
    pallas_call x1, Pallas kernels: 69 us -> 63.8 us  [local(): pl.pallas_call(functools.partial(kernel, sz), name='saddle', out_shape=[p...]
where the time goes in v3:
time: 66.3 us; the launch traced here: 66.1 us
  Pallas kernels  65.3 us (98%)
  between operations  0.8 us (1%)
    pallas_call x1, Pallas kernels, local(): pl.pallas_call(functools.partial(kernel, sz), name='saddle', out_shape=[p...  63.8 us
    pallas_call x1, Pallas kernels, local(): pl.pallas_call(functools.partial(finish, sz), name='finish', out_shape=[b...  1.49 us

profile of v3, /device:TPU:1, one launch (start us, length us, event | category | flops | bytes accessed | tf_op | source)
XLA Modules:
  0.0 66.1 jit_solution(3861522621973037656)
XLA Ops:
  0.6 63.8 %saddle.1 = (f32[16,144,128]{2,1,0:T(8,128)S(1)}, f32[16,144,128]{2,1,0:T(8,128)S(1)}, f32[16,144,128]{2,1,0:T(8,128)S(1)}, f32[16,144,128]{2,1,0:T(8,128)S(1)}, f32[1,128]{1,0:T(1,128)S(1)}) custom-call(f32[1,137,16,128]{3,2,1,0:T(8,128)} %inc_h.1, f32[1,137,16,128]{3,2,1,0:T(8,128)} %dual_h.1, f32[1,137,16,128]{3,2,1,0:T(8,128)} %forc_h.1, ...), custom_call_target="tpu_custom_call" | custom-call | tf_op jit(solution)/shard_map/saddle/pallas_call | solution.py:706
  64.4 1.5 %finish.1 = (f32[1,137,16,128]{3,2,1,0:T(8,128)}, f32[1,137,16,128]{3,2,1,0:T(8,128)}) custom-call(f32[16,144,128]{2,1,0:T(8,128)S(1)} %get-tuple-element.7.forc, f32[16,144,128]{2,1,0:T(8,128)S(1)} %get-tuple-element.8.grad, f32[16,144,128]{2,1,0:T(8,128)S(1)} %get-tuple-element.9.dual, f32[16,144,128]{2,1,0:T(8,128)S(1)} %get-tuple-element.10.inc, ...), custom_call_target="tpu_custom_call" | custom-call | tf_op jit(solution)/shard_map/finish/pallas_call | solution.py:758

commit v4 on v3

--- a/solution.py
+++ b/solution.py
@@ -57,6 +57,12 @@
     group_a = [(dx, dy, dc) for dx in range(XS) for dy in range(sz.gy) for dc in range(2)][1:]
     group_b = [(dh, dl) for dh in range(2) for dl in range(zchips)][1:]
 
+    def hops(p):
+        return min(p[0], XS - p[0]) + min(p[1], sz.gy - p[1]) + 0.5 * p[2]
+
+    group_a.sort(key=hops, reverse=True)
+    group_b.sort(key=lambda p: -p[0])
+
     def peer_a(dx, dy, dc):
         return {
             "tm": zh * XS + lax.rem(xc + dx, XS),
@@ -435,10 +441,10 @@
         with scope(f"halo_y{k}"):
             extra_y()
             recv_y(k)
-        step_edges(which, stencil_edges)
         with scope(f"halo_x{k}"):
             extra_x()
             recv_x(k)
+        step_edges(which, stencil_edges)
         step_outer(k, which, stencil, emit)
         send_x(k + 1)
         for i in range(R // 8):

time: 66.3 us -> 66.2 us (level)
  no operation moved by 1% of the time
where the time goes in v4:
time: 66.2 us; the launch traced here: 66.1 us
  Pallas kernels  65.3 us (99%)
  between operations  0.8 us (1%)
    pallas_call x1, Pallas kernels, local(): pl.pallas_call(functools.partial(kernel, sz), name='saddle', out_shape=[p...  63.8 us
    pallas_call x1, Pallas kernels, local(): pl.pallas_call(functools.partial(finish, sz), name='finish', out_shape=[b...  1.49 us

profile of v4, /device:TPU:1, one launch (start us, length us, event | category | flops | bytes accessed | tf_op | source)
XLA Modules:
  0.0 66.1 jit_solution(8746476283408099712)
XLA Ops:
  0.6 63.8 %saddle.1 = (f32[16,144,128]{2,1,0:T(8,128)S(1)}, f32[16,144,128]{2,1,0:T(8,128)S(1)}, f32[16,144,128]{2,1,0:T(8,128)S(1)}, f32[16,144,128]{2,1,0:T(8,128)S(1)}, f32[1,128]{1,0:T(1,128)S(1)}) custom-call(f32[1,137,16,128]{3,2,1,0:T(8,128)} %inc_h.1, f32[1,137,16,128]{3,2,1,0:T(8,128)} %dual_h.1, f32[1,137,16,128]{3,2,1,0:T(8,128)} %forc_h.1, ...), custom_call_target="tpu_custom_call" | custom-call | tf_op jit(solution)/shard_map/saddle/pallas_call | solution.py:712
  64.4 1.5 %finish.1 = (f32[1,137,16,128]{3,2,1,0:T(8,128)}, f32[1,137,16,128]{3,2,1,0:T(8,128)}) custom-call(f32[16,144,128]{2,1,0:T(8,128)S(1)} %get-tuple-element.7.forc, f32[16,144,128]{2,1,0:T(8,128)S(1)} %get-tuple-element.8.grad, f32[16,144,128]{2,1,0:T(8,128)S(1)} %get-tuple-element.9.dual, f32[16,144,128]{2,1,0:T(8,128)S(1)} %get-tuple-element.10.inc, ...), custom_call_target="tpu_custom_call" | custom-call | tf_op jit(solution)/shard_map/finish/pallas_call | solution.py:764
